TPU v7x, 32 devices: a whole 2x2x4 slice. The times are simulated.
32 devices in a mesh: dp: 8 (over y, x, core), expert: 4 (over z).
Axes of the slice: x: 2, y: 2, z: 4, core: 2. Of those that a mesh axis runs over, the one named last changes fastest.
Arguments:
- hidden_act: bfloat16 [4096, 2048], P('dp', 'expert'), may hold values from -6 to 6
- out_grad: bfloat16 [4096, 7168], P('dp'), may hold values from -0.125 to 0.125
- counts: int32 [8], P('dp'), may hold values from 0 to 512
- expert_master: float32 [7168, 2048], P('dp', 'expert'), may hold values from -0.005 to 0.005
- expert_mom: float32 [7168, 2048], P('dp', 'expert'), may hold values from -0.12 to 0.12
- expert_var: float32 [7168, 2048], P('dp', 'expert'), may hold values from 0.001 to 0.1
- dense_partial: float32 [8, 4, 14336], P('dp', 'expert'), may hold values from -0.8 to 0.8
- dense_master: float32 [14336], replicated, may hold values from 0.5 to 1.5
- dense_mom: float32 [14336], replicated, may hold values from -2 to 2
- dense_var: float32 [14336], replicated, may hold values from 0.1 to 10
Outputs:
- routed_weight: bfloat16 [7168, 2048], P(None, 'expert')
- new_expert_master: float32 [7168, 2048], P('dp', 'expert')
- new_expert_mom: float32 [7168, 2048], P('dp', 'expert')
- new_expert_var: float32 [7168, 2048], P('dp', 'expert')
- new_dense_master: float32 [14336], replicated
- new_dense_mom: float32 [14336], replicated
- new_dense_var: float32 [14336], replicated
All inputs are finite; a program needn't handle non-finite values.
Results may differ from a plain program's by a relative error of at most 0.0004.
Values may be sent and summed in bfloat16 or wider, within the bound.
No kernel may reach another device: no remote copies, remote signals or barrier semaphores. Data moves between devices by JAX's collectives and lax.ppermute only.
A program may use at most 128 MiB of HBM per device.

v0:
```python
import jax
import jax.numpy as jnp
from jax import lax
from jax.sharding import PartitionSpec as P

beta_one = 0.9
beta_two = 0.95
learn_rate = 0.00022
decay_rate = 0.1
epsilon = 1e-08
step_count = 100


def adamw(gradient, master, moment, second):
    moment_new = beta_one * moment + (1.0 - beta_one) * gradient
    second_new = beta_two * second + (1.0 - beta_two) * gradient * gradient
    first_fix = 1.0 - beta_one**step_count
    second_fix = 1.0 - beta_two**step_count
    update = (
        moment_new / first_fix / (jnp.sqrt(second_new / second_fix) + epsilon) + decay_rate * master
    )
    return (master - learn_rate * update, moment_new, second_new)


def on_device(
    hidden_act,
    out_grad,
    counts,
    expert_master,
    expert_mom,
    expert_var,
    dense_partial,
    dense_master,
    dense_mom,
    dense_var,
):
    slots = hidden_act.shape[0]
    row_live = lax.iota(jnp.int32, slots) < counts[0]
    masked = jnp.where(row_live[:, None], hidden_act, jnp.zeros_like(hidden_act))
    dense_local = dense_partial.reshape(-1)
    expert_grad = lax.psum_scatter(
        lax.dot_general(
            out_grad, masked, (((0,), (0,)), ((), ())), preferred_element_type=jnp.float32
        ),
        "dp",
        scatter_dimension=0,
        tiled=True,
    )
    dense_grad = lax.psum(dense_local, ("dp", "expert"))
    dense_new, dense_moment, dense_second = adamw(dense_grad, dense_master, dense_mom, dense_var)
    master_new, moment_new, second_new = adamw(expert_grad, expert_master, expert_mom, expert_var)
    routed_weight = lax.all_gather(master_new.astype(jnp.bfloat16), "dp", axis=0, tiled=True)
    return (
        routed_weight,
        master_new,
        moment_new,
        second_new,
        dense_new,
        dense_moment,
        dense_second,
    )


def solution(mesh):
    in_specs = (
        P("dp", "expert"),
        P("dp", None),
        P("dp"),
        P("dp", "expert"),
        P("dp", "expert"),
        P("dp", "expert"),
        P("dp", "expert", None),
        P(),
        P(),
        P(),
    )
    out_specs = (
        P(None, "expert"),
        P("dp", "expert"),
        P("dp", "expert"),
        P("dp", "expert"),
        P(),
        P(),
        P(),
    )
    return jax.shard_map(
        on_device, mesh=mesh, in_specs=in_specs, out_specs=out_specs, check_vma=False
    )
```

profile of v0, /device:TPU:0, one launch (start us, length us, event | category | flops | bytes accessed | tf_op | source)
XLA Modules:
  0.0 200.4 jit_solution(5589663375833429149)
XLA Ops:
  7.2 0.0 reduce-scatter.2.cloned.1.call-start
  7.9 12.6 %convolution_bitcast_fusion = f32[7168,512]{0,1:T(8,128)} fusion(bf16[512,7168]{1,0:T(8,128)(2,1)} %param.11, bf16[512,512]{1,0:T(8,128)(2,1)} %param.10, pred[512]{0:T(512)(128)(4,1)S(1)} %iota_compare_fusion), kind=kOutput, calls=%fused_computation | convolution fusion | flops 3758358528 | bytes 22544896 | tf_op jit(solution)/shard_map/dot_general | solution.py:42
  20.5 0.0 copy-start
  20.5 0.0 reduce-scatter.2.cloned.1.call-update
  20.5 0.0 all-gather.2.cloned.1.call-start
  20.5 1.4 copy-done
  22.0 1.7 copy.17
  23.6 0.0 copy-start.1
  23.6 2.9 %copy.18 = f32[896,512]{0,1:T(8,128)} copy(f32[896,512]{1,0:T(8,128)} %param.15) | data formatting | bytes 3670016 | tf_op args[5]
  26.5 0.0 copy-done.1
  26.5 1.7 copy.20
  28.2 0.0 copy-start.5
  28.2 0.0 copy-start.2
  28.2 0.0 copy-start.3
  28.2 0.0 copy-start.4
  28.2 97.5 %reduce-scatter.2.cloned.1.call-done = f32[896,512]{0,1:T(8,128)} async-done(((f32[7168,512]{0,1:T(8,128)}), f32[896,512]{0,1:T(8,128)}) %reduce-scatter.2.cloned.1.call-update) | async-done | bytes 1835024 | tf_op jit(solution)/shard_map/reduce_scatter | solution.py:41
  125.6 6.9 %fusion.7 = (bf16[896,512]{0,1:T(8,128)(2,1)}, f32[896,512]{0,1:T(8,128)}, f32[896,512]{0,1:T(8,128)}, f32[896,512]{0,1:T(8,128)S(1)}) fusion(f32[896,512]{0,1:T(8,128)} %copy.20, f32[896,512]{0,1:T(8,128)} %reduce-scatter.2.cloned.1.call-done, f32[896,512]{0,1:T(8,128)} %copy.17, f32[896,512]{0,1:T(8,128)} %copy.18), kind=kLoop, calls=%fused_computation.14 | loop fusion | flops 7340032 | bytes 13762560 | tf_op jit(solution)/shard_map/convert_element_type | solution.py:52
  132.5 0.0 all-gather.2.cloned.1.call-update
  132.5 0.0 copy-done.5
  132.6 40.8 %psum.7 = f32[14336]{0:T(1024)S(1)} all-reduce(f32[14336]{0:T(1024)S(1)} %bitcast.6), channel_id=1, replica_groups=mesh['dp'=8,'expert'=4] {'dp','expert'}, use_global_device_ids=true, to_apply=%region_1.2 | all-reduce | flops 14336 | bytes 114688 | tf_op jit(solution)/shard_map/psum | solution.py:49
  173.3 0.0 copy-done.2
  173.3 0.0 copy-done.3
  173.3 0.0 copy-done.4
  173.3 0.7 multiply_subtract_fusion.1
  174.0 2.7 %copy.22 = f32[896,512]{1,0:T(8,128)} copy(f32[896,512]{0,1:T(8,128)} %get-tuple-element.18) | data formatting | bytes 3670016
  176.8 2.7 %copy.23 = f32[896,512]{1,0:T(8,128)} copy(f32[896,512]{0,1:T(8,128)} %get-tuple-element.19) | data formatting | bytes 3670016
  179.5 1.7 copy.24
  181.1 2.0 all-gather.2.cloned.1.call-done
  183.1 10.4 %copy.21 = bf16[7168,512]{1,0:T(8,128)(2,1)} copy(bf16[7168,512]{0,1:T(8,128)(2,1)} %all-gather.2.cloned.1.call-done) | data formatting | bytes 14680064
  (1 shorter events, 0.0 us)
Async XLA Ops:
  7.2 118.5 %reduce-scatter.2.cloned.1.call-start = ((), (), s32[]{:S(2)}) async-start(), calls=%async_computation.1 | async-start | bytes 16515072 | tf_op jit(solution)/shard_map/reduce_scatter | solution.py:41
  20.5 1.5 copy-start
  20.5 162.6 %all-gather.2.cloned.1.call-start = ((), (), s32[]{:S(2)}) async-start(), calls=%async_computation.2 | async-start | bytes 8257536 | tf_op jit(solution)/shard_map/all_gather | solution.py:52
  23.6 2.9 %copy-start.1 = (f32[896,512]{1,0:T(8,128)S(1)}, f32[896,512]{1,0:T(8,128)}, u32[]{:S(2)}) copy-start(f32[896,512]{1,0:T(8,128)} %param.13) | copy-start | bytes 5505028
  28.2 104.4 %copy-start.5 = (f32[1,1,14336]{2,1,0:T(1,128)S(1)}, f32[1,1,14336]{2,1,0:T(1,128)}, u32[]{:S(2)}) copy-start(f32[1,1,14336]{2,1,0:T(1,128)} %param.16) | copy-start | bytes 172036
  28.2 145.2 %copy-start.2 = (f32[14336]{0:T(1024)S(1)}, f32[14336]{0:T(1024)}, u32[]{:S(2)}) copy-start(f32[14336]{0:T(1024)} %param.17) | copy-start | bytes 172036
  28.2 145.2 %copy-start.3 = (f32[14336]{0:T(1024)S(1)}, f32[14336]{0:T(1024)}, u32[]{:S(2)}) copy-start(f32[14336]{0:T(1024)} %param.18) | copy-start | bytes 172036
  28.2 145.2 %copy-start.4 = (f32[14336]{0:T(1024)S(1)}, f32[14336]{0:T(1024)}, u32[]{:S(2)}) copy-start(f32[14336]{0:T(1024)} %param.19) | copy-start | bytes 172036
Sparse Core Ops, SparseCore 0:
  20.6 104.9 reduce-scatter.1
  132.7 50.4 all-gather.1
where the time goes:
time: 201 us; the launch traced here: 200 us
  waiting for transfers between devices  99.5 us (50%)
  blocking collectives  40.8 us (20%)
  local copies, waits for them, and re-layouts  25.2 us (13%)
  between operations  14.7 us (7%)
  matrix products  12.6 us (6%)
  other arithmetic  7.57 us (4%)
    reduce_scatter x1, waiting for transfers between devices, on_device(): lax.psum_scatter(lax.dot_general(out_grad, masked, (((0,), (0,)), ((), ()...  97.5 us
    psum x1, blocking collectives, on_device(): dense_grad = lax.psum(dense_local, ('dp', 'expert'))  40.8 us
    unnamed x19, local copies, waits for them, and re-layouts  25.2 us
    dot_general x1, matrix products, on_device(): lax.dot_general(out_grad, masked, (((0,), (0,)), ((), ())), preferred_ele...  12.6 us
    convert_element_type x1, other arithmetic, on_device(): master_new.astype(jnp.bfloat16)  6.88 us
  transfers between devices with their start and end apart: 2, of which 2 were waited for; matrix products, arithmetic and copies ran while one was open for 7% of the time, Pallas kernels for 0%

commit v1 on v0

--- a/solution.py
+++ b/solution.py
@@ -46,7 +46,7 @@
         scatter_dimension=0,
         tiled=True,
     )
-    dense_grad = lax.psum(dense_local, ("dp", "expert"))
+    dense_grad = jnp.sum(lax.all_gather(dense_local, ("dp", "expert")), axis=0)
     dense_new, dense_moment, dense_second = adamw(dense_grad, dense_master, dense_mom, dense_var)
     master_new, moment_new, second_new = adamw(expert_grad, expert_master, expert_mom, expert_var)
     routed_weight = lax.all_gather(master_new.astype(jnp.bfloat16), "dp", axis=0, tiled=True)

time: 201 us -> 205 us (1.020)
  blocking collectives: 40.8 us -> 0 us
  waiting for transfers between devices: 99.5 us -> 140 us
  other arithmetic: 7.57 us -> 10.1 us
    psum x1 -> x0, blocking collectives: 40.8 us -> none  [on_device(): dense_grad = lax.psum(dense_local, ('dp', 'expert'))]
    all_gather x1, waiting for transfers between devices: 1.97 us -> 39 us  [on_device(): lax.all_gather(master_new.astype(jnp.bfloat16), 'dp', axis=0, tiled=True)]
    reduce_scatter x1, waiting for transfers between devices: 97.5 us -> 101 us  [on_device(): lax.psum_scatter(lax.dot_general(out_grad, masked, (((0,), (0,)), ((), ()...]
    reduce_sum x0 -> x1, other arithmetic: none -> 2.55 us  [on_device(): dense_grad = jnp.sum(lax.all_gather(dense_local, ('dp', 'expert')), axis=0)]
    unnamed x19 -> x17, local copies, waits for them, and re-layouts: 25.2 us -> 24.7 us
  transfers between devices with their start and end apart: 2 -> 3, of which waited for: 2 -> 2; matrix products, arithmetic and copies ran while one was open for 7% -> 12% of each run, Pallas kernels for 0% -> 0%
where the time goes in v1:
time: 205 us; the launch traced here: 204 us
  waiting for transfers between devices  140 us (68%)
  local copies, waits for them, and re-layouts  24.7 us (12%)
  between operations  16.2 us (8%)
  matrix products  12.6 us (6%)
  other arithmetic  10.1 us (5%)
    reduce_scatter x1, waiting for transfers between devices, on_device(): lax.psum_scatter(lax.dot_general(out_grad, masked, (((0,), (0,)), ((), ()...  101 us
    all_gather x1, waiting for transfers between devices, on_device(): lax.all_gather(master_new.astype(jnp.bfloat16), 'dp', axis=0, tiled=True)  39 us
    unnamed x17, local copies, waits for them, and re-layouts  24.7 us
    dot_general x1, matrix products, on_device(): lax.dot_general(out_grad, masked, (((0,), (0,)), ((), ())), preferred_ele...  12.6 us
    convert_element_type x1, other arithmetic, on_device(): master_new.astype(jnp.bfloat16)  6.89 us
  transfers between devices with their start and end apart: 3, of which 2 were waited for; matrix products, arithmetic and copies ran while one was open for 12% of the time, Pallas kernels for 0%

profile of v1, /device:TPU:0, one launch (start us, length us, event | category | flops | bytes accessed | tf_op | source)
XLA Modules:
  0.0 204.2 jit_solution(8898652529132397248)
XLA Ops:
  8.0 0.0 reduce-scatter.2.cloned.1.call-start
  8.7 12.6 %convolution_bitcast_fusion = f32[7168,512]{0,1:T(8,128)} fusion(bf16[512,7168]{1,0:T(8,128)(2,1)} %param.11, bf16[512,512]{1,0:T(8,128)(2,1)} %param.10, pred[512]{0:T(512)(128)(4,1)S(1)} %iota_compare_fusion), kind=kOutput, calls=%fused_computation | convolution fusion | flops 3758358528 | bytes 22544896 | tf_op jit(solution)/shard_map/dot_general | solution.py:42
  21.3 0.0 copy-start
  21.3 0.0 reduce-scatter.2.cloned.1.call-update
  21.3 0.0 all-gather.6.cloned.1.call-start
  21.4 0.5 all-gather.6.cloned.1.call-update
  21.9 0.0 all-gather.4.cloned.1.call-start
  21.9 0.8 copy-done
  22.8 1.7 copy.25
  24.5 0.0 copy-start.1
  24.5 2.9 %copy.26 = f32[896,512]{0,1:T(8,128)} copy(f32[896,512]{1,0:T(8,128)} %param.15) | data formatting | bytes 3670016 | tf_op args[5]
  27.3 0.0 copy-done.1
  27.3 1.7 copy.28
  29.0 100.8 %reduce-scatter.2.cloned.1.call-done = f32[896,512]{0,1:T(8,128)} async-done(((f32[7168,512]{0,1:T(8,128)}), f32[896,512]{0,1:T(8,128)}) %reduce-scatter.2.cloned.1.call-update) | async-done | bytes 1835024 | tf_op jit(solution)/shard_map/reduce_scatter | solution.py:41
  129.8 6.9 %fusion.7 = (bf16[896,512]{0,1:T(8,128)(2,1)}, f32[896,512]{0,1:T(8,128)}, f32[896,512]{0,1:T(8,128)}, f32[896,512]{0,1:T(8,128)S(1)}) fusion(f32[896,512]{0,1:T(8,128)} %copy.28, f32[896,512]{0,1:T(8,128)} %reduce-scatter.2.cloned.1.call-done, f32[896,512]{0,1:T(8,128)} %copy.25, f32[896,512]{0,1:T(8,128)} %copy.26), kind=kLoop, calls=%fused_computation.14 | loop fusion | flops 7340032 | bytes 13762560 | tf_op jit(solution)/shard_map/convert_element_type | solution.py:52
  136.7 0.0 copy-start.2
  136.7 0.0 copy-start.3
  136.7 0.0 copy-start.4
  136.7 0.0 all-gather.4.cloned.1.call-update
  136.7 0.0 all-gather.6.cloned.1.call-done
  136.8 2.6 %reduce_sum.9 = f32[14336]{0:T(1024)S(1)} reduce(f32[32,1,14336]{2,1,0:T(1,128)} %all-gather.6.cloned.1.call-done, f32[]{:T(128)} %constant.5.clone.1), dimensions={0,1}, to_apply=%region_1.2 | reduce | flops 444416 | bytes 1892356 | tf_op jit(solution)/shard_map/reduce_sum | solution.py:49
  139.3 0.0 copy-done.2
  139.3 0.0 copy-done.3
  139.3 0.0 copy-done.4
  139.4 0.7 multiply_subtract_fusion.1
  140.0 2.7 %copy.30 = f32[896,512]{1,0:T(8,128)} copy(f32[896,512]{0,1:T(8,128)} %get-tuple-element.25) | data formatting | bytes 3670016
  142.8 2.9 %copy.31 = f32[896,512]{1,0:T(8,128)} copy(f32[896,512]{0,1:T(8,128)} %get-tuple-element.26) | data formatting | bytes 3670016
  145.6 1.7 copy.32
  147.3 39.0 %all-gather.4.cloned.1.call-done = bf16[7168,512]{0,1:T(8,128)(2,1)} async-done(((bf16[896,512]{0,1:T(8,128)(2,1)}), bf16[7168,512]{0,1:T(8,128)(2,1)}) %all-gather.4.cloned.1.call-update) | async-done | bytes 7340048 | tf_op jit(solution)/shard_map/all_gather | solution.py:52
  186.4 10.4 %copy.29 = bf16[7168,512]{1,0:T(8,128)(2,1)} copy(bf16[7168,512]{0,1:T(8,128)(2,1)} %all-gather.4.cloned.1.call-done) | data formatting | bytes 14680064
  (1 shorter events, 0.0 us)
Async XLA Ops:
  8.0 121.8 %reduce-scatter.2.cloned.1.call-start = ((), (), s32[]{:S(2)}) async-start(), calls=%async_computation.1 | async-start | bytes 16515072 | tf_op jit(solution)/shard_map/reduce_scatter | solution.py:41
  21.3 1.5 copy-start
  21.3 115.4 %all-gather.6.cloned.1.call-start = ((), (), s32[]{:S(2)}) async-start(), calls=%async_computation.3 | async-start | bytes 1892352 | tf_op jit(solution)/shard_map/all_gather | solution.py:49
  21.9 164.5 %all-gather.4.cloned.1.call-start = ((), (), s32[]{:S(2)}) async-start(), calls=%async_computation.2 | async-start | bytes 8257536 | tf_op jit(solution)/shard_map/all_gather | solution.py:52
  24.5 2.9 %copy-start.1 = (f32[896,512]{1,0:T(8,128)S(1)}, f32[896,512]{1,0:T(8,128)}, u32[]{:S(2)}) copy-start(f32[896,512]{1,0:T(8,128)} %param.13) | copy-start | bytes 5505028
  136.7 2.6 %copy-start.2 = (f32[14336]{0:T(1024)S(1)}, f32[14336]{0:T(1024)}, u32[]{:S(2)}) copy-start(f32[14336]{0:T(1024)} %param.17) | copy-start | bytes 172036
  136.7 2.6 %copy-start.3 = (f32[14336]{0:T(1024)S(1)}, f32[14336]{0:T(1024)}, u32[]{:S(2)}) copy-start(f32[14336]{0:T(1024)} %param.18) | copy-start | bytes 172036
  136.7 2.6 %copy-start.4 = (f32[14336]{0:T(1024)S(1)}, f32[14336]{0:T(1024)}, u32[]{:S(2)}) copy-start(f32[14336]{0:T(1024)} %param.19) | copy-start | bytes 172036
Sparse Core Ops, SparseCore 0:
  21.4 108.3 reduce-scatter.1
Sparse Core Ops, SparseCore 1:
  24.6 73.8 all-gather.5
  136.8 49.5 all-gather.3
